TPU v7x, 256 devices: a whole 4x4x8 slice. The times are simulated.
256 devices in a mesh: expert: 16 (over x, y), dp: 16 (over z, core).
Axes of the slice: x: 4, y: 4, z: 8, core: 2. Of those that a mesh axis runs over, the one named last changes fastest.
Arguments:
- tokens: bfloat16 [2, 32768, 1280], P(None, ('expert', 'dp')), may hold values from -6 to 6
- modality: int32 [2, 32768], P(None, ('expert', 'dp')), may hold values from 0 to 1, as said below
- routes: int32 [2, 32768, 1], P(None, ('expert', 'dp')), may hold values from 0 to 15; in each aligned block of 128 rows (0 to 127, 128 to 255, ..., all dimensions but the last counted through in order) at most 16 rows name the same one
- router: bfloat16 [1280, 16], replicated, may hold values from -0.15625 to 0.15625
- w_in: bfloat16 [16, 1280, 5120], P('expert', 'dp'), may hold values from -0.15625 to 0.15625
- w_out: bfloat16 [16, 5120, 1280], P('expert', 'dp'), may hold values from -0.078125 to 0.078125
Outputs:
- mixed: bfloat16 [2, 32768, 1280], P(None, ('expert', 'dp'))
- load: float32 [2, 2, 16], replicated
Inputs may be any that keep to these rules, and one draw needn't show every extreme that they name: `routes`: among the 128 tokens of one micro-batch on one device (aligned blocks of 128 rows), at most 16 are routed to any one expert. `modality`: in every aligned block of 128 tokens of a micro-batch, the number of text tokens lies between 32 and 96.
All inputs are finite; a program needn't handle non-finite values.
Results may differ from a plain program's by a relative error of at most 0.0057.
Values may be sent and summed in bfloat16 or wider, within the bound.
No kernel may reach another device: no remote copies, remote signals or barrier semaphores. Data moves between devices by JAX's collectives and lax.ppermute only.
A program may use at most 192 MiB of HBM per device.

v0:
```python
import jax
import jax.numpy as jnp
from jax import lax
from jax.sharding import Mesh
from jax.sharding import PartitionSpec as P

EXPERT = ("expert_0", "expert_1")
DP = ("dp_0", "dp_1")
EXPERT_DP = ("expert_0", "expert_1", "dp_0", "dp_1")


def over_axes(shard, axes):
    for axis in axes:
        shard = lax.psum(shard, axis)
    return shard


def on_device(tokens, modality, routes, router, w_in, w_out):
    micro_count, tok_count, model_width = tokens.shape
    experts = router.shape[1]
    capacity = 2 * tok_count // experts
    logits = jnp.einsum("mtd,de->mte", tokens, router, preferred_element_type=jnp.float32)
    onehot = (routes == jnp.arange(experts, dtype=jnp.int32)[None, None, :]).astype(jnp.float32)
    gating = jax.nn.sigmoid(jnp.sum(logits * onehot, axis=-1))
    running = jnp.cumsum(onehot, axis=1)
    slot_pos = jnp.sum((running - 1.0) * onehot, axis=-1)
    slot_hot = (
        slot_pos[:, :, None] == jnp.arange(capacity, dtype=jnp.float32)[None, None, :]
    ).astype(jnp.float32)
    placer = (onehot[:, :, :, None] * slot_hot[:, :, None, :]).reshape(
        micro_count, tok_count, experts * capacity
    )
    placer = placer.astype(jnp.bfloat16)
    buffer = jnp.einsum("mtk,mtd->mkd", placer, tokens, preferred_element_type=jnp.float32)
    buffer = buffer.astype(jnp.bfloat16).reshape(micro_count, experts, capacity, model_width)
    arrived = lax.all_to_all(buffer, EXPERT, split_axis=1, concat_axis=1, tiled=True)
    token_rows = arrived.reshape(-1, model_width)
    columns = token_rows
    pre_act = jnp.dot(
        columns, lax.all_gather(w_in, DP, axis=1, tiled=True)[0], preferred_element_type=jnp.float32
    )
    hidden = jax.nn.gelu(pre_act, approximate=True).astype(jnp.bfloat16)
    columns = hidden
    served = jnp.dot(
        columns,
        lax.all_gather(w_out, DP, axis=1, tiled=True)[0],
        preferred_element_type=jnp.float32,
    )
    served = served.astype(jnp.bfloat16).reshape(arrived.shape)
    returned = lax.all_to_all(served, EXPERT, split_axis=1, concat_axis=1, tiled=True)
    returned = returned.reshape(micro_count, experts * capacity, model_width)
    combined = jnp.einsum("mtk,mkd->mtd", placer, returned, preferred_element_type=jnp.float32)
    mixed = (combined * gating[:, :, None]).astype(jnp.bfloat16)
    exps = jnp.exp(logits)
    router_probs = exps / jnp.sum(exps, axis=-1, keepdims=True)
    modal_hot = (modality[:, :, None] == jnp.arange(2, dtype=jnp.int32)[None, None, :]).astype(
        jnp.float32
    )
    counts = jnp.einsum("mtk,mte->ke", modal_hot, onehot, precision=lax.Precision.HIGHEST)
    prob_sums = jnp.einsum("mtk,mte->ke", modal_hot, router_probs, precision=lax.Precision.HIGHEST)
    modal_counts = jnp.sum(modal_hot, axis=(0, 1))
    counts, prob_sums, modal_counts = (
        over_axes(counts, EXPERT_DP),
        over_axes(prob_sums, EXPERT_DP),
        over_axes(modal_counts, EXPERT_DP),
    )
    load = jnp.stack(
        [experts * counts / modal_counts[:, None], experts * prob_sums / modal_counts[:, None]]
    )
    return (mixed, load)


def solution(mesh):
    torus = Mesh(mesh.devices.reshape(4, 4, 8, 2), ("expert_0", "expert_1", "dp_0", "dp_1"))
    in_specs = (
        P(None, EXPERT_DP, None),
        P(None, EXPERT_DP),
        P(None, EXPERT_DP, None),
        P(),
        P(EXPERT, DP, None),
        P(EXPERT, DP, None),
    )
    out_specs = (P(None, EXPERT_DP, None), P())
    return jax.shard_map(
        on_device, mesh=torus, in_specs=in_specs, out_specs=out_specs, check_vma=False
    )
```

profile of v0, /device:TPU:1, one launch (start us, length us, event | category | flops | bytes accessed | tf_op | source)
XLA Modules:
  0.0 258.7 jit_solution(4837752513307506845)
XLA Ops:
  7.2 0.0 copy-start
  7.2 0.0 all-gather.5.cloned.1.call-start
  7.2 0.7 all-gather.5.cloned.1.call-update
  7.9 0.0 all-gather.3.cloned.1.call-start
  8.0 0.7 all-gather.3.cloned.1.call-update
  8.7 0.7 fusion.30
  9.3 0.1 copy.21
  9.5 0.2 reduce_window_sum.11
  9.6 0.1 copy.22
  9.7 0.8 fusion.29
  10.5 0.5 convolution_convert_fusion
  11.0 0.1 copy.23
  11.1 26.3 %all_to_all.10 = bf16[2,16,16,1280]{3,2,0,1:T(8,128)(2,1)S(1)} all-to-all(bf16[2,16,16,1280]{3,2,0,1:T(8,128)(2,1)S(1)} %copy.23), channel_id=1, replica_groups=mesh['expert_0'=4,'expert_1'=4,'dp_0'=8,'dp_1'=2] {'expert_0','expert_1'}, dimensions={1} | all-to-all | bytes 2621440 | tf_op jit(solution)/shard_map/all_to_all | solution.py:36
  37.5 0.1 copy.24
  37.6 54.6 %all-gather.5.cloned.1.call-done = bf16[1,5120,1280]{2,1,0:T(8,128)(2,1)} async-done(((bf16[1,320,1280]{2,1,0:T(8,128)(2,1)}), bf16[1,5120,1280]{2,1,0:T(8,128)(2,1)}) %all-gather.5.cloned.1.call-update) | async-done | bytes 13107216 | tf_op jit(solution)/shard_map/all_gather | solution.py:46
  92.1 78.5 %all-gather.3.cloned.1.call-done = bf16[1,1280,5120]{2,1,0:T(8,128)(2,1)} async-done(((bf16[1,80,5120]{2,1,0:T(8,128)(2,1)}), bf16[1,1280,5120]{2,1,0:T(8,128)(2,1)}) %all-gather.3.cloned.1.call-update) | async-done | bytes 13107216 | tf_op jit(solution)/shard_map/all_gather | solution.py:40
  170.6 22.4 %fusion.20 = bf16[512,1280]{1,0:T(8,128)(2,1)S(1)} fusion(bf16[1,5120,1280]{2,1,0:T(8,128)(2,1)} %all-gather.5.cloned.1.call-done, bf16[512,1280]{1,0:T(8,128)(2,1)S(1)} %bitcast.41, bf16[1,1280,5120]{2,1,0:T(8,128)(2,1)} %all-gather.3.cloned.1.call-done), kind=kOutput, calls=%fused_computation.17 | convolution fusion | flops 13446021120 | bytes 28835840 | tf_op jit(solution)/shard_map/dot_general | solution.py:44
  193.0 0.0 copy-start.3
  193.0 1.2 copy.25
  194.2 6.5 %all-to-all-start.1 = ((bf16[2,16,16,1280]{3,2,0,1:T(8,128)(2,1)}), bf16[2,16,16,1280]{3,2,0,1:T(8,128)(2,1)S(1)}, u32[]{:S(2)}, u32[]{:S(2)}) async-start(bf16[2,16,16,1280]{3,2,0,1:T(8,128)(2,1)} %copy.25), calls=%async_computation.1 | async-start | bytes 2621440 | tf_op jit(solution)/shard_map/all_to_all | solution.py:50
  200.8 0.1 convert_reduce_fusion
  200.9 0.1 convolution_bitcast_fusion.1
  201.0 0.3 exponential_reduce_fusion
  201.4 0.1 convolution_bitcast_fusion
  201.5 18.4 %all-reduce.2 = (f32[2,16]{1,0:T(2,128)S(1)}, f32[2]{0:T(128)S(1)}, f32[2,16]{1,0:T(2,128)S(1)}) all-reduce(f32[2,16]{1,0:T(2,128)S(1)} %convolution_bitcast_fusion, f32[2]{0:T(128)S(1)} %convert_reduce_fusion, f32[2,16]{1,0:T(2,128)S(1)} %convolution_bitcast_fusion.1), channel_id=1, replica_groups=mesh['expert_0'=4,'expert_1'=4,'dp_0'=8,'dp_1'=2] {'expert_0'}, use_global_device_ids=true, to_apply=%region_13.14 | all-reduce | flops 66 | bytes 528 | tf_op jit(solution)/shard_map/psum | solution.py:14
  219.9 8.1 %all-reduce.1 = (f32[2,16]{1,0:T(2,128)S(1)}, f32[2]{0:T(128)S(1)}, f32[2,16]{1,0:T(2,128)S(1)}) all-reduce(f32[2,16]{1,0:T(2,128)S(1)} %get-tuple-element.10, f32[2]{0:T(128)S(1)} %get-tuple-element.11, f32[2,16]{1,0:T(2,128)S(1)} %get-tuple-element.12), channel_id=1, replica_groups=mesh['expert_0'=4,'expert_1'=4,'dp_0'=8,'dp_1'=2] {'expert_1'}, use_global_device_ids=true, to_apply=%region_14.15 | all-reduce | flops 66 | bytes 528 | tf_op jit(solution)/shard_map/psum | solution.py:14
  227.9 11.8 %all-reduce = (f32[2,16]{1,0:T(2,128)S(1)}, f32[2]{0:T(128)S(1)}, f32[2,16]{1,0:T(2,128)S(1)}) all-reduce(f32[2,16]{1,0:T(2,128)S(1)} %get-tuple-element.7, f32[2]{0:T(128)S(1)} %get-tuple-element.8, f32[2,16]{1,0:T(2,128)S(1)} %get-tuple-element.9), channel_id=1, replica_groups=mesh['expert_0'=4,'expert_1'=4,'dp_0'=8,'dp_1'=2] {'dp_0'}, use_global_device_ids=true, to_apply=%region_15.16 | all-reduce | flops 66 | bytes 528 | tf_op jit(solution)/shard_map/psum | solution.py:14
  239.7 10.2 %all-reduce.3 = (f32[2,16]{1,0:T(2,128)S(1)}, f32[2]{0:T(128)S(1)}, f32[2,16]{1,0:T(2,128)S(1)}) all-reduce(f32[2,16]{1,0:T(2,128)S(1)} %get-tuple-element.4, f32[2]{0:T(128)S(1)} %get-tuple-element.5, f32[2,16]{1,0:T(2,128)S(1)} %get-tuple-element.6), channel_id=1, replica_groups=mesh['expert_0'=4,'expert_1'=4,'dp_0'=8,'dp_1'=2] {'dp_1'}, use_global_device_ids=true, to_apply=%region_16.17 | all-reduce | flops 66 | bytes 528 | tf_op jit(solution)/shard_map/psum | solution.py:14
  249.9 0.1 divide_bitcast_fusion.1
  249.9 0.6 pad_maximum_fusion
  250.5 0.1 copy.26
  250.6 1.2 fusion.25
  (9 shorter events, 0.1 us)
Async XLA Ops:
  7.2 3.3 %copy-start = (bf16[2,128,1280]{2,1,0:T(8,128)(2,1)S(1)}, bf16[2,128,1280]{2,1,0:T(8,128)(2,1)}, u32[]{:S(2)}) copy-start(bf16[2,128,1280]{2,1,0:T(8,128)(2,1)} %param.6) | copy-start | bytes 1966084
  7.2 84.9 %all-gather.5.cloned.1.call-start = ((), (), s32[]{:S(2)}) async-start(), calls=%async_computation.3 | async-start | bytes 13926400 | tf_op jit(solution)/shard_map/all_gather | solution.py:46
  7.9 162.7 %all-gather.3.cloned.1.call-start = ((), (), s32[]{:S(2)}) async-start(), calls=%async_computation.2 | async-start | bytes 13926400 | tf_op jit(solution)/shard_map/all_gather | solution.py:40
  193.0 7.8 %copy-start.3 = (s32[2,128]{1,0:T(2,128)S(1)}, s32[2,128]{1,0:T(2,128)}, u32[]{:S(2)}) copy-start(s32[2,128]{1,0:T(2,128)} %param.7) | copy-start | bytes 3076
  193.0 7.9 %copy-start.2 = (s32[2,128,1]{1,2,0:T(1,128)S(1)}, s32[2,128,1]{1,2,0:T(1,128)}, u32[]{:S(2)}) copy-start(s32[2,128,1]{1,2,0:T(1,128)} %param.8) | copy-start | bytes 3076
  193.0 8.0 %copy-start.1 = (bf16[1280,16]{0,1:T(8,128)(2,1)S(1)}, bf16[1280,16]{0,1:T(8,128)(2,1)}, u32[]{:S(2)}) copy-start(bf16[1280,16]{0,1:T(8,128)(2,1)} %param.9) | copy-start | bytes 122884
  194.2 56.3 %all-to-all-start.1 = ((bf16[2,16,16,1280]{3,2,0,1:T(8,128)(2,1)}), bf16[2,16,16,1280]{3,2,0,1:T(8,128)(2,1)S(1)}, u32[]{:S(2)}, u32[]{:S(2)}) async-start(bf16[2,16,16,1280]{3,2,0,1:T(8,128)(2,1)} %copy.25), calls=%async_computation.1 | async-start | bytes 2621440 | tf_op jit(solution)/shard_map/all_to_all | solution.py:50
Sparse Core Ops, SparseCore 0:
  9.8 82.2 all-gather.4
  93.9 76.5 all-gather.2
where the time goes:
time: 259 us
  waiting for transfers between devices  134 us (52%)
  blocking collectives  74.7 us (29%)
  matrix products  24.7 us (10%)
  between operations  14.2 us (5%)
  starting transfers between devices  6.6 us (3%)
    all_gather x1, waiting for transfers between devices, on_device(): lax.all_gather(w_in, DP, axis=1, tiled=True)[0]  78.5 us
    all_gather x1, waiting for transfers between devices, on_device(): lax.all_gather(w_out, DP, axis=1, tiled=True)[0]  54.6 us
    psum x4, blocking collectives, over_axes(): shard = lax.psum(shard, axis)  48.4 us
    all_to_all x1, blocking collectives, on_device(): lax.all_to_all(buffer, EXPERT, split_axis=1, concat_axis=1, tiled=True)  26.3 us
    dot_general x1, matrix products, on_device(): jnp.dot(columns, lax.all_gather(w_out, DP, axis=1, tiled=True)[0], prefer...  22.4 us
    all_to_all x1, starting transfers between devices, on_device(): lax.all_to_all(served, EXPERT, split_axis=1, concat_axis=1, tiled=True)  6.52 us
  transfers between devices with their start and end apart: 3, of which 2 were waited for; matrix products, arithmetic and copies ran while one was open for 2% of the time, Pallas kernels for 0%

commit v1 on v0

--- a/solution.py
+++ b/solution.py
@@ -33,7 +33,10 @@
     placer = placer.astype(jnp.bfloat16)
     buffer = jnp.einsum("mtk,mtd->mkd", placer, tokens, preferred_element_type=jnp.float32)
     buffer = buffer.astype(jnp.bfloat16).reshape(micro_count, experts, capacity, model_width)
-    arrived = lax.all_to_all(buffer, EXPERT, split_axis=1, concat_axis=1, tiled=True)
+    arrived = jnp.concatenate(
+        lax.all_to_all(jnp.stack(jnp.split(buffer, lax.axis_size(EXPERT), axis=1)), EXPERT, 0, 0),
+        axis=1,
+    )
     token_rows = arrived.reshape(-1, model_width)
     columns = token_rows
     pre_act = jnp.dot(

time: 259 us -> 259 us (level)
    all_gather x1, waiting for transfers between devices: 54.6 us -> 78.5 us  [on_device(): lax.all_gather(w_out, DP, axis=1, tiled=True)[0]]
    all_gather x1, waiting for transfers between devices: 78.5 us -> 55.8 us  [on_device(): lax.all_gather(w_in, DP, axis=1, tiled=True)[0]]
  transfers between devices with their start and end apart: 3 -> 3, of which waited for: 2 -> 2; matrix products, arithmetic and copies ran while one was open for 2% -> 1% of each run, Pallas kernels for 0% -> 0%
where the time goes in v1:
time: 259 us
  waiting for transfers between devices  136 us (53%)
  blocking collectives  74.7 us (29%)
  matrix products  24.9 us (10%)
  between operations  14.3 us (6%)
  starting transfers between devices  6.73 us (3%)
    all_gather x1, waiting for transfers between devices, on_device(): lax.all_gather(w_out, DP, axis=1, tiled=True)[0]  78.5 us
    all_gather x1, waiting for transfers between devices, on_device(): lax.all_gather(w_in, DP, axis=1, tiled=True)[0]  55.8 us
    psum x4, blocking collectives, over_axes(): shard = lax.psum(shard, axis)  48.4 us
    all_to_all x1, blocking collectives, on_device(): lax.all_to_all(jnp.stack(jnp.split(buffer, lax.axis_size(EXPERT), axis=1)...  26.3 us
    dot_general x1, matrix products, on_device(): jnp.dot(columns, lax.all_gather(w_out, DP, axis=1, tiled=True)[0], prefer...  22.6 us
    all_to_all x1, starting transfers between devices, on_device(): lax.all_to_all(served, EXPERT, split_axis=1, concat_axis=1, tiled=True)  6.66 us
  transfers between devices with their start and end apart: 3, of which 2 were waited for; matrix products, arithmetic and copies ran while one was open for 1% of the time, Pallas kernels for 0%

profile of v1, /device:TPU:1, one launch (start us, length us, event | category | flops | bytes accessed | tf_op | source)
XLA Modules:
  0.0 259.0 jit_solution(8694648168887669077)
XLA Ops:
  7.2 0.0 copy-start
  7.2 0.0 copy-start.2
  7.2 0.0 all-gather.3.cloned.1.call-start
  7.2 0.7 all-gather.3.cloned.1.call-update
  7.9 0.0 all-gather.5.cloned.1.call-start
  8.0 0.7 all-gather.5.cloned.1.call-update
  8.7 0.1 copy.46
  8.8 0.2 reduce_window_sum.11
  9.0 0.1 copy.47
  9.0 0.1 fusion.45
  9.2 0.5 convolution_convert_fusion
  9.9 26.3 %all_to_all.10 = bf16[16,2,1,16,1280]{4,3,1,2,0:T(8,128)(2,1)S(1)} all-to-all(bf16[16,2,1,16,1280]{4,3,1,2,0:T(8,128)(2,1)S(1)} %fusion.26), channel_id=1, replica_groups=mesh['expert_0'=4,'expert_1'=4,'dp_0'=8,'dp_1'=2] {'expert_0','expert_1'}, dimensions={0} | all-to-all | bytes 2621440 | tf_op jit(solution)/shard_map/all_to_all | solution.py:37
  36.2 0.1 copy.64
  36.3 55.8 %all-gather.3.cloned.1.call-done = bf16[1,1280,5120]{2,1,0:T(8,128)(2,1)} async-done(((bf16[1,80,5120]{2,1,0:T(8,128)(2,1)}), bf16[1,1280,5120]{2,1,0:T(8,128)(2,1)}) %all-gather.3.cloned.1.call-update) | async-done | bytes 13107216 | tf_op jit(solution)/shard_map/all_gather | solution.py:43
  92.1 78.5 %all-gather.5.cloned.1.call-done = bf16[1,5120,1280]{2,1,0:T(8,128)(2,1)} async-done(((bf16[1,320,1280]{2,1,0:T(8,128)(2,1)}), bf16[1,5120,1280]{2,1,0:T(8,128)(2,1)}) %all-gather.5.cloned.1.call-update) | async-done | bytes 13107216 | tf_op jit(solution)/shard_map/all_gather | solution.py:49
  170.6 22.6 %fusion.20 = bf16[512,1280]{1,0:T(8,128)(2,1)S(1)} fusion(bf16[1,5120,1280]{2,1,0:T(8,128)(2,1)} %all-gather.5.cloned.1.call-done, bf16[512,1280]{1,0:T(8,128)(2,1)S(1)} %bitcast.154, bf16[1,1280,5120]{2,1,0:T(8,128)(2,1)} %all-gather.3.cloned.1.call-done), kind=kOutput, calls=%fused_computation.17 | convolution fusion | flops 13446021120 | bytes 28835840 | tf_op jit(solution)/shard_map/dot_general | solution.py:47
  193.2 1.2 copy.65
  194.4 6.7 %all-to-all-start.1 = ((bf16[2,16,16,1280]{3,2,0,1:T(8,128)(2,1)}), bf16[2,16,16,1280]{3,2,0,1:T(8,128)(2,1)S(1)}, u32[]{:S(2)}, u32[]{:S(2)}) async-start(bf16[2,16,16,1280]{3,2,0,1:T(8,128)(2,1)} %copy.65), calls=%async_computation.1 | async-start | bytes 2621440 | tf_op jit(solution)/shard_map/all_to_all | solution.py:53
  201.1 0.0 copy-done.3
  201.1 0.1 convert_reduce_fusion
  201.2 0.1 convolution_bitcast_fusion.1
  201.3 0.3 exponential_reduce_fusion
  201.7 0.1 convolution_bitcast_fusion
  201.8 18.4 %all-reduce.2 = (f32[2,16]{1,0:T(2,128)S(1)}, f32[2]{0:T(128)S(1)}, f32[2,16]{1,0:T(2,128)S(1)}) all-reduce(f32[2,16]{1,0:T(2,128)S(1)} %convolution_bitcast_fusion, f32[2]{0:T(128)S(1)} %convert_reduce_fusion, f32[2,16]{1,0:T(2,128)S(1)} %convolution_bitcast_fusion.1), channel_id=1, replica_groups=mesh['expert_0'=4,'expert_1'=4,'dp_0'=8,'dp_1'=2] {'expert_0'}, use_global_device_ids=true, to_apply=%region_13.14 | all-reduce | flops 66 | bytes 528 | tf_op jit(solution)/shard_map/psum | solution.py:14
  220.2 8.1 %all-reduce.1 = (f32[2,16]{1,0:T(2,128)S(1)}, f32[2]{0:T(128)S(1)}, f32[2,16]{1,0:T(2,128)S(1)}) all-reduce(f32[2,16]{1,0:T(2,128)S(1)} %get-tuple-element.10, f32[2]{0:T(128)S(1)} %get-tuple-element.11, f32[2,16]{1,0:T(2,128)S(1)} %get-tuple-element.12), channel_id=1, replica_groups=mesh['expert_0'=4,'expert_1'=4,'dp_0'=8,'dp_1'=2] {'expert_1'}, use_global_device_ids=true, to_apply=%region_14.15 | all-reduce | flops 66 | bytes 528 | tf_op jit(solution)/shard_map/psum | solution.py:14
  228.2 11.8 %all-reduce = (f32[2,16]{1,0:T(2,128)S(1)}, f32[2]{0:T(128)S(1)}, f32[2,16]{1,0:T(2,128)S(1)}) all-reduce(f32[2,16]{1,0:T(2,128)S(1)} %get-tuple-element.7, f32[2]{0:T(128)S(1)} %get-tuple-element.8, f32[2,16]{1,0:T(2,128)S(1)} %get-tuple-element.9), channel_id=1, replica_groups=mesh['expert_0'=4,'expert_1'=4,'dp_0'=8,'dp_1'=2] {'dp_0'}, use_global_device_ids=true, to_apply=%region_15.16 | all-reduce | flops 66 | bytes 528 | tf_op jit(solution)/shard_map/psum | solution.py:14
  240.0 10.2 %all-reduce.3 = (f32[2,16]{1,0:T(2,128)S(1)}, f32[2]{0:T(128)S(1)}, f32[2,16]{1,0:T(2,128)S(1)}) all-reduce(f32[2,16]{1,0:T(2,128)S(1)} %get-tuple-element.4, f32[2]{0:T(128)S(1)} %get-tuple-element.5, f32[2,16]{1,0:T(2,128)S(1)} %get-tuple-element.6), channel_id=1, replica_groups=mesh['expert_0'=4,'expert_1'=4,'dp_0'=8,'dp_1'=2] {'dp_1'}, use_global_device_ids=true, to_apply=%region_16.17 | all-reduce | flops 66 | bytes 528 | tf_op jit(solution)/shard_map/psum | solution.py:14
  250.2 0.1 divide_bitcast_fusion.1
  250.2 0.6 pad_maximum_fusion
  250.8 0.0 all-to-all-done.1
  250.8 0.1 copy.66
  250.9 1.2 fusion.25
  (24 shorter events, 0.2 us)
Async XLA Ops:
  7.2 2.0 copy-start
  7.2 1.5 copy-start.2
  7.2 84.9 %all-gather.3.cloned.1.call-start = ((), (), s32[]{:S(2)}) async-start(), calls=%async_computation.2 | async-start | bytes 13926400 | tf_op jit(solution)/shard_map/all_gather | solution.py:43
  7.9 162.7 %all-gather.5.cloned.1.call-start = ((), (), s32[]{:S(2)}) async-start(), calls=%async_computation.3 | async-start | bytes 13926400 | tf_op jit(solution)/shard_map/all_gather | solution.py:49
  194.4 6.7 %copy-start.3 = (s32[2,128]{1,0:T(2,128)S(1)}, s32[2,128]{1,0:T(2,128)}, u32[]{:S(2)}) copy-start(s32[2,128]{1,0:T(2,128)} %param.7) | copy-start | bytes 3076
  194.4 6.9 %copy-start.1 = (bf16[1280,16]{0,1:T(8,128)(2,1)S(1)}, bf16[1280,16]{0,1:T(8,128)(2,1)}, u32[]{:S(2)}) copy-start(bf16[1280,16]{0,1:T(8,128)(2,1)} %param.9) | copy-start | bytes 122884
  194.4 56.4 %all-to-all-start.1 = ((bf16[2,16,16,1280]{3,2,0,1:T(8,128)(2,1)}), bf16[2,16,16,1280]{3,2,0,1:T(8,128)(2,1)S(1)}, u32[]{:S(2)}, u32[]{:S(2)}) async-start(bf16[2,16,16,1280]{3,2,0,1:T(8,128)(2,1)} %copy.65), calls=%async_computation.1 | async-start | bytes 2621440 | tf_op jit(solution)/shard_map/all_to_all | solution.py:53
Sparse Core Ops, SparseCore 0:
  9.8 82.2 all-gather.2
  94.0 76.5 all-gather.4
